TPU v7x, 128 devices: a whole 4x4x4 slice. The times are simulated.
128 devices in a mesh: cand: 8 (over y, core), feat: 16 (over x, z).
Axes of the slice: x: 4, y: 4, z: 4, core: 2. Of those that a mesh axis runs over, the one named last changes fastest.
Arguments:
- embeddings: bfloat16 [262144, 4096], P('cand', 'feat'), may hold values from -1 to 1
- winners: int32 [3], replicated, may hold values from 0 to 262143, as said below
Outputs:
- gains: float32 [262144], P('cand')
- coords: float32 [3, 262144], P(None, 'cand')
- best: float32 [3], replicated
Inputs may be any that keep to these rules, and one draw needn't show every extreme that they name: `winners`: 3 different candidates.
All inputs are finite; a program needn't handle non-finite values.
Results may differ from a plain program's by a relative error of at most 0.0003.
Values may be sent and summed in bfloat16 or wider, within the bound.
A program may use at most 128 MiB of HBM per device.

v0:
```python
import jax
import jax.numpy as jnp
from jax import lax
from jax.sharding import PartitionSpec as P

STEPS = 3


def copy_for_each(x, axis):
    count = lax.axis_size(axis)
    return lax.all_to_all(jnp.broadcast_to(x[None], (count, *x.shape)), axis, 0, 0, tiled=True)


def over_copies(x, axis):
    return copy_for_each(x, axis).sum(axis=0)


def split_up(x, dim, count):
    before, after = (x.shape[:dim], x.shape[dim + 1 :])
    return jnp.moveaxis(x.reshape(*before, count, -1, *after), dim, 0)


def summed_on_arrival(x, axis, dim):
    count = lax.axis_size(axis)
    pieces = lax.all_to_all(split_up(x, dim, count), axis, 0, 0, tiled=True)
    return jnp.sum(pieces, axis=0)


def rows_for(lines, count):
    spare = -len(lines) % count
    return jnp.pad(lines, [(0, spare)] + [(0, 0)] * (lines.ndim - 1))


def joined_along(pieces, dim):
    shape = list(pieces.shape[1:])
    shape[dim] *= pieces.shape[0]
    return jnp.moveaxis(pieces, 0, dim).reshape(shape)


def gather_directly(x, axis, dim):
    pieces = copy_for_each(x, axis)
    return joined_along(pieces, dim)


def sum_by_parts(x, axes):
    own = summed_on_arrival(rows_for(x, lax.axis_size(axes)), axes, 0)
    whole = gather_directly(own, axes, 0)
    return whole[: len(x)].reshape(x.shape)


def packed_total(arrays, axis):
    ravelled, at, done = (jnp.concatenate([a.reshape(-1) for a in arrays]), 0, [])
    subtotal = sum_by_parts(ravelled, axis)
    for a in arrays:
        done.append(subtotal[at : at + a.size].reshape(a.shape))
        at += a.size
    return tuple(done)


def taken_together(x, axis):
    everything = copy_for_each(x, axis)
    return jnp.max(everything, axis=0)


def per_device(embeddings, winners):
    cand_rows = embeddings.shape[0]
    here = lax.axis_index("cand")
    partial_norms = jnp.sum(jnp.square(embeddings.astype(jnp.float32)), axis=1)
    coords = []
    owners = winners // cand_rows
    locals_idx = winners % cand_rows
    picked = jnp.take(embeddings, locals_idx, axis=0).astype(jnp.float32)
    mine = (owners == here)[:, None]
    stacked = jnp.where(mine, picked, jnp.zeros_like(picked))
    rows_win = over_copies(stacked, "cand").astype(jnp.bfloat16)
    partial_dots = lax.dot_general(
        rows_win, embeddings, (((1,), (1,)), ((), ())), preferred_element_type=jnp.float32
    )
    partial_gram = lax.dot_general(
        rows_win, rows_win, (((1,), (1,)), ((), ())), preferred_element_type=jnp.float32
    )
    dots, gram, norms = packed_total((partial_dots, partial_gram, partial_norms), "feat")
    gains = norms
    winner_coords = [[None] * STEPS for step in range(STEPS)]
    winner_gains = [gram[step, step] for step in range(STEPS)]
    step_best = []
    for step in range(STEPS):
        scale = jnp.sqrt(jnp.maximum(winner_gains[step], 1.0))
        proj = jnp.zeros((cand_rows,), jnp.float32)
        for prior in range(step):
            proj = proj + coords[prior] * winner_coords[step][prior]
        fresh = (dots[step] - proj) / scale
        gains = gains - fresh * fresh
        coords.append(fresh)
        step_best.append(jnp.max(gains))
        for later in range(step + 1, STEPS):
            inner = jnp.zeros((), jnp.float32)
            for prior in range(step):
                inner = winner_coords[later][prior] * winner_coords[step][prior]
            value = (gram[later, step] - inner) / scale
            winner_coords[later][step] = value
            winner_gains[later] = winner_gains[later] - value * value
    best_all = taken_together(jnp.stack(step_best), "cand")
    coords_all = jnp.stack(coords)
    return (gains, coords_all, best_all)


def solution(mesh):
    return jax.shard_map(
        per_device,
        mesh=mesh,
        in_specs=(P("cand", "feat"), P()),
        out_specs=(P("cand"), P(None, "cand"), P()),
        check_vma=False,
    )
```

profile of v0, /device:TPU:1, one launch (start us, length us, event | category | flops | bytes accessed | tf_op | source)
XLA Modules:
  0.0 107.1 jit_solution(14940802164871375500)
XLA Ops:
  0.6 0.7 compare_and_fusion
  1.3 8.5 %gather_fusion = bf16[3,256]{1,0:T(4,128)(2,1)S(1)} fusion(bf16[32768,256]{1,0:T(8,128)(2,1)} %param.2, s32[1024]{0:T(1024)S(1)} %pad_clamp_fusion), kind=kCustom, calls=%fused_computation | custom fusion | bytes 3084 | tf_op jit(solution)/shard_map/jit(_take)/gather | solution.py:72
  9.9 0.6 broadcast_in_dim.47
  10.5 6.0 %all-to-all-start = ((f32[8,3,256]{2,1,0:T(4,128)}), f32[8,3,256]{2,1,0:T(4,128)S(1)}, u32[]{:S(2)}, u32[]{:S(2)}) async-start(f32[8,3,256]{2,1,0:T(4,128)} %broadcast_in_dim.47), calls=%async_computation | async-start | bytes 65536 | tf_op jit(solution)/shard_map/all_to_all | solution.py:11
  16.5 7.6 %multiply_reduce_fusion = f32[32768]{0:T(1024)S(1)} fusion(bf16[32768,256]{1,0:T(8,128)(2,1)} %param.2), kind=kLoop, calls=%fused_computation.1 | loop fusion | flops 25133056 | bytes 16908288 | tf_op jit(solution)/shard_map/reduce_sum | solution.py:68
  24.1 10.2 %fusion.14 = f32[3,32768]{1,0:T(4,128)S(1)} fusion(bf16[3,256]{1,0:T(4,128)(2,1)S(1)} %reduce_sum.27, bf16[32768,256]{1,0:T(8,128)(2,1)} %param.2), kind=kOutput, calls=%fused_computation.31 | convolution fusion | flops 50331648 | bytes 17171968 | tf_op jit(solution)/shard_map/dot_general | solution.py:76
  34.4 0.3 reshape.91
  34.8 1.0 concatenate.3
  35.8 0.7 all_to_all.18
  36.5 18.8 %all_to_all.26 = f32[16,1,8193]{2,1,0:T(1,128)S(1)} all-to-all(f32[16,1,8193]{2,1,0:T(1,128)S(1)} %all_to_all.18), channel_id=1, replica_groups=mesh['cand'=8,'feat'=16] {'feat'}, dimensions={0} | all-to-all | bytes 1048704 | tf_op jit(solution)/shard_map/all_to_all | solution.py:25
  55.3 0.3 reduce_sum.29
  55.7 0.3 broadcast_in_dim.48
  55.9 13.3 %all_to_all.27 = f32[16,1,8193]{2,1,0:T(1,128)S(1)} all-to-all(f32[16,1,8193]{2,1,0:T(1,128)S(1)} %broadcast_in_dim.48), channel_id=1, replica_groups=mesh['cand'=8,'feat'=16] {'feat'}, dimensions={0} | all-to-all | bytes 1048704 | tf_op jit(solution)/shard_map/all_to_all | solution.py:11
  69.3 1.3 %reduce.2 = f32[16,8193]{1,0:T(8,128)S(1)} reduce(f32[16,1,8193]{2,1,0:T(1,128)S(1)} %all_to_all.27, f32[]{:T(128)} %constant.60), dimensions={1}, to_apply=%all_to_all.20.reduce_sub_computation | reduce | bytes 1048708 | tf_op jit(solution)/shard_map/all_to_all | solution.py:11
  70.5 14.4 %slice.53 = f32[43696,3]{1,0:T(8,128)} reshape(f32[16,8193]{1,0:T(8,128)S(1)} %reduce.2) | data formatting | bytes 1048704 | tf_op jit(solution)/shard_map/slice | solution.py:55
  84.9 1.5 %fusion.12 = (f32[1,1]{1,0:T(1,128)}, f32[1,1]{1,0:T(1,128)}, f32[1,1]{1,0:T(1,128)}, f32[1,1]{1,0:T(1,128)}, f32[1,1]{1,0:T(1,128)}, /*index=5*/f32[1,1]{1,0:T(1,128)}) fusion(f32[43696,3]{1,0:T(8,128)} %slice.53), kind=kLoop, calls=%fused_computation.29 | loop fusion | bytes 48 | tf_op jit(solution)/shard_map/slice | solution.py:100
  90.7 0.7 fusion.8
  91.4 1.4 %fusion.10 = (f32[]{:T(128)}, f32[32768]{0:T(1024)}, f32[32768]{0:T(1024)S(1)}) fusion(f32[32768]{0:T(1024)S(1)} %get-tuple-element.5, f32[32768]{0:T(1024)S(1)} %get-tuple-element.6, f32[131088]{0:T(1024)S(1)} %reshape.93, f32[]{:T(128)S(6)} %sqrt.15, f32[]{:T(128)S(6)} %div.64, f32[]{:T(128)S(6)} %div.63), kind=kLoop, calls=%fused_computation.28 | loop fusion | flops 393215 | bytes 786448 | tf_op jit(solution)/shard_map/reduce_max | solution.py:95
  92.8 2.1 %pad_maximum_fusion.1 = f32[3]{0:T(128)S(1)} fusion(f32[1]{0:T(128)} %bitcast.11, f32[1]{0:T(128)} %bitcast.10, f32[1]{0:T(128)} %bitcast.9), kind=kLoop, calls=%fused_computation.25 | loop fusion | flops 6 | bytes 24 | tf_op jit(solution)/shard_map/stack | solution.py:103
  94.9 0.6 broadcast_in_dim.49
  95.5 6.5 %all-to-all-start.3 = ((f32[8,1,3]{2,1,0:T(1,128)}), f32[8,1,3]{2,1,0:T(1,128)S(1)}, u32[]{:S(2)}, u32[]{:S(2)}) async-start(f32[8,1,3]{2,1,0:T(1,128)} %broadcast_in_dim.49), calls=%async_computation.3 | async-start | bytes 8192 | tf_op jit(solution)/shard_map/all_to_all | solution.py:11
  102.0 1.1 %pad_maximum_fusion = f32[3,32768]{1,0:T(4,128)} fusion(f32[1,32768]{1,0:T(1,128)S(1)} %bitcast.18, f32[1,32768]{1,0:T(1,128)S(1)} %bitcast.16, f32[1,32768]{1,0:T(1,128)S(1)} %bitcast.17), kind=kLoop, calls=%fused_computation.2 | loop fusion | flops 196608 | bytes 786432 | tf_op jit(solution)/shard_map/stack | solution.py:104
  103.1 3.5 %all-to-all-done.3 = f32[8,1,3]{2,1,0:T(1,128)S(1)} async-done(((f32[8,1,3]{2,1,0:T(1,128)}), f32[8,1,3]{2,1,0:T(1,128)S(1)}, u32[]{:S(2)}, u32[]{:S(2)}) %all-to-all-start.3) | async-done | bytes 128 | tf_op jit(solution)/shard_map/all_to_all | solution.py:11
  106.6 0.5 reduce_max.39
  (8 shorter events, 0.6 us)
Async XLA Ops:
  10.5 13.6 %all-to-all-start = ((f32[8,3,256]{2,1,0:T(4,128)}), f32[8,3,256]{2,1,0:T(4,128)S(1)}, u32[]{:S(2)}, u32[]{:S(2)}) async-start(f32[8,3,256]{2,1,0:T(4,128)} %broadcast_in_dim.47), calls=%async_computation | async-start | bytes 65536 | tf_op jit(solution)/shard_map/all_to_all | solution.py:11
  95.5 11.1 %all-to-all-start.3 = ((f32[8,1,3]{2,1,0:T(1,128)}), f32[8,1,3]{2,1,0:T(1,128)S(1)}, u32[]{:S(2)}, u32[]{:S(2)}) async-start(f32[8,1,3]{2,1,0:T(1,128)} %broadcast_in_dim.49), calls=%async_computation.3 | async-start | bytes 8192 | tf_op jit(solution)/shard_map/all_to_all | solution.py:11
where the time goes:
time: 108 us; the launch traced here: 107 us
  blocking collectives  32.1 us (30%)
  local copies, waits for them, and re-layouts  28.3 us (26%)
  other arithmetic  15.8 us (15%)
  starting transfers between devices  12.5 us (12%)
  matrix products  10.3 us (10%)
  between operations  4.68 us (4%)
  waiting for transfers between devices  3.47 us (3%)
    all_to_all x1, blocking collectives, summed_on_arrival(): pieces = lax.all_to_all(split_up(x, dim, count), axis, 0, 0, tiled=True)  18.8 us
    slice x1, local copies, waits for them, and re-layouts, packed_total(): done.append(subtotal[at:at + a.size].reshape(a.shape))  14.4 us
    all_to_all x1, blocking collectives, copy_for_each(): lax.all_to_all(jnp.broadcast_to(x[None], (count, *x.shape)), axis, 0, 0,...  13.3 us
    all_to_all x2, starting transfers between devices, copy_for_each(): lax.all_to_all(jnp.broadcast_to(x[None], (count, *x.shape)), axis, 0, 0,...  12.5 us
    dot_general x1, matrix products, per_device(): lax.dot_general(rows_win, embeddings, (((1,), (1,)), ((), ())), preferred...  10.2 us
    gather x1, local copies, waits for them, and re-layouts, per_device(): picked = jnp.take(embeddings, locals_idx, axis=0).astype(jnp.float32)  8.49 us
    reduce_sum x1, other arithmetic, per_device(): partial_norms = jnp.sum(jnp.square(embeddings.astype(jnp.float32)), axis=1)  7.59 us
    all_to_all x2, waiting for transfers between devices, copy_for_each(): lax.all_to_all(jnp.broadcast_to(x[None], (count, *x.shape)), axis, 0, 0,...  3.47 us
  transfers between devices with their start and end apart: 2, of which 1 were waited for; matrix products, arithmetic and copies ran while one was open for 8% of the time, Pallas kernels for 0%

commit v1 on v0

v1 whole, which is shorter than its diff:
```python
import jax
import jax.numpy as jnp
from jax import lax
from jax.experimental import pallas as pl
from jax.experimental.pallas import tpu as pltpu
from jax.sharding import PartitionSpec as P

MESH = pl.DeviceIdType.MESH
STEPS = 3
CAND = 8
SIDE = 4
FEAT = SIDE * SIDE
ROWS = 32768
WIDTH = 256
HALF = ROWS // 2
QUART = HALF // SIDE
PIECE = QUART // SIDE
CHUNKS = 16
CHUNK = ROWS // CHUNKS
TILE = 512


def nt_dot(a, b):
    return lax.dot_general(a, b, (((1,), (1,)), ((), ())), preferred_element_type=jnp.float32)


def pick_kernel(win_ref, emb_ref, out_ref, blocks, sems):
    here = lax.axis_index("cand")
    copies = []
    for k in range(STEPS):
        row = lax.rem(win_ref[k], ROWS)
        start = pl.multiple_of(lax.div(row, 16) * 16, 16)
        copy = pltpu.make_async_copy(emb_ref.at[pl.ds(start, 16), :], blocks.at[k], sems.at[k])
        copy.start()
        copies.append(copy)
    out_ref[...] = jnp.zeros_like(out_ref)
    lines = lax.broadcasted_iota(jnp.int32, (16, WIDTH), 0)
    for k in range(STEPS):
        copies[k].wait()
        owner = lax.div(win_ref[k], ROWS)
        line = jnp.where(owner == here, lax.rem(win_ref[k], 16), -1)
        block = blocks[k].astype(jnp.float32)
        kept = jnp.where(lines == line, block, 0.0)
        out_ref[k : k + 1, :] = jnp.sum(kept, axis=0, keepdims=True)


def main_kernel(
    rows_ref, emb_ref, out_ref, best_ref,
    emb, part, won, gram_own, grams, in_a, in_b, sum_a, sum_b, in_c, in_d, whole, top, tops_c, tops_f,
    emb_sem, won_s, won_r, gram_s, gram_r, a_s, a_r, b_s, b_r, c_s, c_r, d_s, d_r,
    e_s, e_r, f_s, f_r, g_s, g_r, h_s, h_r, tc_s, tc_r, tf_s, tf_r, out_sem,
):
    c = lax.axis_index("cand")
    f = lax.axis_index("feat")
    x = lax.div(f, SIDE)
    z = lax.rem(f, SIDE)

    def load(i):
        lines = pl.ds(pl.multiple_of(i * CHUNK, CHUNK), CHUNK)
        return pltpu.make_async_copy(emb_ref.at[lines, :], emb.at[lines, :], emb_sem.at[i])

    for i in range(CHUNKS):
        load(i).start()

    def cand_peer(k):
        return (lax.rem(c + k, CAND), f)

    def x_peer(k):
        return (c, lax.rem(x + k, SIDE) * SIDE + z)

    def z_peer(k):
        return (c, x * SIDE + lax.rem(z + k, SIDE))

    def feat_peer(k):
        return (c, lax.rem(f + k, FEAT))

    def send(src, dst, s, r, k, peer):
        return pltpu.make_async_remote_copy(
            src_ref=src, dst_ref=dst, send_sem=s.at[k - 1], recv_sem=r.at[k - 1],
            device_id=peer, device_id_type=MESH,
        )

    barrier = pltpu.get_barrier_semaphore()
    for k in range(1, CAND):
        pl.semaphore_signal(barrier, inc=1, device_id=cand_peer(k), device_id_type=MESH)
    for k in range(1, FEAT):
        pl.semaphore_signal(barrier, inc=1, device_id=feat_peer(k), device_id_type=MESH)
    pl.semaphore_wait(barrier, CAND - 1 + FEAT - 1)

    won_out = [send(rows_ref, won.at[k - 1], won_s, won_r, k, cand_peer(k)) for k in range(1, CAND)]
    for copy in won_out:
        copy.start()

    ones = jnp.where(lax.broadcasted_iota(jnp.int32, (8, WIDTH), 0) == 3, 1.0, 0.0).astype(jnp.bfloat16)

    def norm_chunk(i, _):
        load(i).wait()

        def norm_tile(j, _):
            at = pl.multiple_of(i * CHUNK + j * TILE, TILE)
            e = emb[pl.ds(at, TILE), :].astype(jnp.float32)
            sq = e * e
            s = sq[:, :128] + sq[:, 128:]
            high = s.astype(jnp.bfloat16)
            low = (s - high.astype(jnp.float32)).astype(jnp.bfloat16)
            line = nt_dot(ones, jnp.concatenate([high, low], axis=1))
            part[:, pl.ds(at, TILE)] = line[0:4, :]
            return 0

        return lax.fori_loop(0, CHUNK // TILE, norm_tile, 0)

    lax.fori_loop(0, CHUNKS, norm_chunk, 0)

    for copy in won_out:
        copy.wait()
    total = rows_ref[...]
    for k in range(CAND - 1):
        total = total + won[k]
    w = total.astype(jnp.bfloat16)

    gram_own[...] = nt_dot(w, jnp.concatenate([w] * 16, axis=0))
    gram_out = [send(gram_own, grams.at[k - 1], gram_s, gram_r, k, feat_peer(k)) for k in range(1, FEAT)]
    for copy in gram_out:
        copy.start()

    def dots(base):
        def dot_tile(j, _):
            at = pl.multiple_of(base + j * TILE, TILE)
            line = nt_dot(w, emb[pl.ds(at, TILE), :])
            part[0:3, pl.ds(at, TILE)] = line[0:3, :]
            return 0

        lax.fori_loop(0, QUART // TILE, dot_tile, 0)

    def a_cols(xi):
        return pl.multiple_of(xi * QUART, QUART)

    def b_cols(zi):
        return pl.multiple_of(HALF + zi * QUART, QUART)

    first = []
    for k in (2, 1, 3, 0):
        at = a_cols(lax.rem(x + k, SIDE))
        dots(at)
        if k:
            copy = send(part.at[:, pl.ds(at, QUART)], in_a.at[k - 1], a_s, a_r, k, x_peer(k))
            copy.start()
            first.append(copy)
        at = b_cols(lax.rem(z + k, SIDE))
        dots(at)
        if k:
            copy = send(part.at[:, pl.ds(at, QUART)], in_b.at[k - 1], b_s, b_r, k, z_peer(k))
            copy.start()
            first.append(copy)
    for copy in first:
        copy.wait()

    second = []
    for k in (2, 1, 3, 0):
        zi = lax.rem(z + k, SIDE)
        here = pl.ds(pl.multiple_of(zi * PIECE, PIECE), PIECE)
        own = pl.ds(pl.multiple_of(a_cols(x) + zi * PIECE, PIECE), PIECE)
        sum_a[:, here] = part[:, own] + in_a[0, :, here] + in_a[1, :, here] + in_a[2, :, here]
        if k:
            copy = send(sum_a.at[:, here], in_c.at[k - 1], c_s, c_r, k, z_peer(k))
            copy.start()
            second.append(copy)
        xi = lax.rem(x + k, SIDE)
        here = pl.ds(pl.multiple_of(xi * PIECE, PIECE), PIECE)
        own = pl.ds(pl.multiple_of(b_cols(z) + xi * PIECE, PIECE), PIECE)
        sum_b[:, here] = part[:, own] + in_b[0, :, here] + in_b[1, :, here] + in_b[2, :, here]
        if k:
            copy = send(sum_b.at[:, here], in_d.at[k - 1], d_s, d_r, k, x_peer(k))
            copy.start()
            second.append(copy)

    for copy in gram_out:
        copy.wait()
    gram = gram_own[...]
    for k in range(FEAT - 1):
        gram = gram + grams[k]
    own_gain = [gram[s : s + 1, s : s + 1] for s in range(STEPS)]
    own_coord = [[None] * STEPS for _ in range(STEPS)]
    inverse = []
    for s in range(STEPS):
        inverse.append(1.0 / jnp.sqrt(jnp.maximum(own_gain[s], 1.0)))
        for later in range(s + 1, STEPS):
            value = gram[later : later + 1, s : s + 1]
            for prior in range(s):
                value = value - own_coord[later][prior] * own_coord[s][prior]
            value = value * inverse[s]
            own_coord[later][s] = value
            own_gain[later] = own_gain[later] - value * value

    for copy in second:
        copy.wait()

    def finish(sums, base, arrived, out_at):
        here = pl.ds(base, PIECE)
        t = sums[:, here] + arrived[0] + arrived[1] + arrived[2]
        gains = t[3:4, :]
        coords = []
        bests = []
        for s in range(STEPS):
            proj = t[s : s + 1, :]
            if s:
                back = jnp.zeros_like(proj)
                for prior in range(s):
                    back = back + coords[prior] * own_coord[s][prior]
                proj = proj - back
            fresh = proj * inverse[s]
            gains = gains - fresh * fresh
            coords.append(fresh)
            bests.append(jnp.max(gains, axis=1, keepdims=True))
            whole[s : s + 1, pl.ds(out_at, PIECE)] = fresh
        whole[3:4, pl.ds(out_at, PIECE)] = gains
        return bests

    own_a = pl.multiple_of(a_cols(x) + z * PIECE, PIECE)
    own_b = pl.multiple_of(b_cols(z) + x * PIECE, PIECE)
    best_a = finish(sum_a, pl.multiple_of(z * PIECE, PIECE), in_c, own_a)
    best_b = finish(sum_b, pl.multiple_of(x * PIECE, PIECE), in_d, own_b)
    lines = lax.broadcasted_iota(jnp.int32, (8, 128), 0)
    mine = jnp.zeros((8, 128), jnp.float32)
    for s in range(STEPS):
        mine = jnp.where(lines == s, jnp.maximum(best_a[s], best_b[s]), mine)
    top[0] = mine
    top_out = [send(top.at[0], tops_c.at[k - 1], tc_s, tc_r, k, cand_peer(k)) for k in range(1, CAND)]
    for copy in top_out:
        copy.start()

    third = []
    for k in (2, 1, 3):
        here = pl.ds(own_a, PIECE)
        copy = send(whole.at[:, here], whole.at[:, here], e_s, e_r, k, z_peer(k))
        copy.start()
        third.append(copy)
        here = pl.ds(own_b, PIECE)
        copy = send(whole.at[:, here], whole.at[:, here], f_s, f_r, k, x_peer(k))
        copy.start()
        third.append(copy)

    for copy in top_out:
        copy.wait()
    for k in range(CAND - 1):
        mine = jnp.maximum(mine, tops_c[k])
    top[1] = mine
    top_out = [send(top.at[1], tops_f.at[k - 1], tf_s, tf_r, k, feat_peer(k)) for k in range(1, FEAT)]
    for copy in top_out:
        copy.start()

    for copy in third:
        copy.wait()
    fourth = []
    for k in (2, 1, 3):
        here = pl.ds(a_cols(x), QUART)
        copy = send(whole.at[:, here], whole.at[:, here], g_s, g_r, k, x_peer(k))
        copy.start()
        fourth.append(copy)
        here = pl.ds(b_cols(z), QUART)
        copy = send(whole.at[:, here], whole.at[:, here], h_s, h_r, k, z_peer(k))
        copy.start()
        fourth.append(copy)
    for copy in top_out:
        copy.wait()
    for k in range(FEAT - 1):
        mine = jnp.maximum(mine, tops_f[k])
    best_ref[...] = mine
    for copy in fourth:
        copy.wait()
    done = pltpu.make_async_copy(whole, out_ref, out_sem)
    done.start()
    done.wait()


def per_device(embeddings, winners):
    rows = pl.pallas_call(
        pick_kernel,
        out_shape=jax.ShapeDtypeStruct((8, WIDTH), jnp.float32),
        in_specs=[pl.BlockSpec(memory_space=pltpu.SMEM), pl.BlockSpec(memory_space=pl.ANY)],
        out_specs=pl.BlockSpec(memory_space=pltpu.VMEM),
        scratch_shapes=[pltpu.VMEM((STEPS, 16, WIDTH), jnp.bfloat16), pltpu.SemaphoreType.DMA((STEPS,))],
        name="pick",
    )(winners, embeddings)
    f32 = jnp.float32
    sem = pltpu.SemaphoreType.DMA
    ring = [sem((SIDE - 1,)), sem((SIDE - 1,))]
    out, best = pl.pallas_call(
        main_kernel,
        out_shape=(jax.ShapeDtypeStruct((4, ROWS), f32), jax.ShapeDtypeStruct((8, 128), f32)),
        in_specs=[pl.BlockSpec(memory_space=pltpu.VMEM), pl.BlockSpec(memory_space=pl.ANY)],
        out_specs=(pl.BlockSpec(memory_space=pl.ANY), pl.BlockSpec(memory_space=pltpu.VMEM)),
        scratch_shapes=[
            pltpu.VMEM((ROWS, WIDTH), jnp.bfloat16),
            pltpu.VMEM((4, ROWS), f32),
            pltpu.VMEM((CAND - 1, 8, WIDTH), f32),
            pltpu.VMEM((8, 128), f32),
            pltpu.VMEM((FEAT - 1, 8, 128), f32),
            pltpu.VMEM((SIDE - 1, 4, QUART), f32),
            pltpu.VMEM((SIDE - 1, 4, QUART), f32),
            pltpu.VMEM((4, QUART), f32),
            pltpu.VMEM((4, QUART), f32),
            pltpu.VMEM((SIDE - 1, 4, PIECE), f32),
            pltpu.VMEM((SIDE - 1, 4, PIECE), f32),
            pltpu.VMEM((4, ROWS), f32),
            pltpu.VMEM((2, 8, 128), f32),
            pltpu.VMEM((CAND - 1, 8, 128), f32),
            pltpu.VMEM((FEAT - 1, 8, 128), f32),
            sem((CHUNKS,)),
            sem((CAND - 1,)), sem((CAND - 1,)),
            sem((FEAT - 1,)), sem((FEAT - 1,)),
            *ring, *ring, *ring, *ring, *ring, *ring, *ring, *ring,
            sem((CAND - 1,)), sem((CAND - 1,)),
            sem((FEAT - 1,)), sem((FEAT - 1,)),
            sem,
        ],
        compiler_params=pltpu.CompilerParams(
            collective_id=0, has_side_effects=True, vmem_limit_bytes=40 * 1024 * 1024
        ),
        name="main",
    )(rows, embeddings)
    return (out[3], out[:3], best[:STEPS, 0])


def solution(mesh):
    return jax.shard_map(
        per_device,
        mesh=mesh,
        in_specs=(P("cand", "feat"), P()),
        out_specs=(P("cand"), P(None, "cand"), P()),
        check_vma=False,
    )
```

time: 108 us -> 54.2 us (0.50)
  Pallas kernels: 0 us -> 50.3 us
  blocking collectives: 32.1 us -> 0 us
  local copies, waits for them, and re-layouts: 28.3 us -> 2.9 us
  other arithmetic: 15.8 us -> 0 us
  starting transfers between devices: 12.5 us -> 0 us
  matrix products: 10.3 us -> 0 us
  between operations: 4.68 us -> 0.66 us
  waiting for transfers between devices: 3.47 us -> 0 us
    pallas_call x0 -> x2, Pallas kernels: none -> 50.3 us  [the longest x1 48.3 us: per_device(): pl.pallas_call(main_kernel, out_shape=(jax.ShapeDtypeStruct((4, ROWS), f3...]
    all_to_all x2 -> x0, blocking collectives: 32.1 us -> none  [the longest x1 18.8 us: summed_on_arrival(): pieces = lax.all_to_all(split_up(x, dim, count), axis, 0, 0, tiled=True)]
    slice x2, local copies, waits for them, and re-layouts: 15.9 us -> 1.42 us  [per_device(): return (out[3], out[:3], best[:STEPS, 0])]
    all_to_all x2 -> x0, starting transfers between devices: 12.5 us -> none  [copy_for_each(): lax.all_to_all(jnp.broadcast_to(x[None], (count, *x.shape)), axis, 0, 0,...]
    dot_general x2 -> x0, matrix products: 10.3 us -> none  [the longest x1 10.2 us: per_device(): lax.dot_general(rows_win, embeddings, (((1,), (1,)), ((), ())), preferred...]
    gather x1 -> x0, local copies, waits for them, and re-layouts: 8.49 us -> none  [per_device(): picked = jnp.take(embeddings, locals_idx, axis=0).astype(jnp.float32)]
    reduce_sum x3 -> x0, other arithmetic: 7.95 us -> none  [the longest x1 7.59 us: per_device(): partial_norms = jnp.sum(jnp.square(embeddings.astype(jnp.float32)), axis=1)]
    all_to_all x2 -> x0, waiting for transfers between devices: 3.47 us -> none  [copy_for_each(): lax.all_to_all(jnp.broadcast_to(x[None], (count, *x.shape)), axis, 0, 0,...]
  transfers between devices with their start and end apart: 2 -> 0, of which waited for: 1 -> 0; matrix products, arithmetic and copies ran while one was open for 8% -> 0% of each run, Pallas kernels for 0% -> 0%
where the time goes in v1:
time: 54.2 us; the launch traced here: 53.9 us
  Pallas kernels  50.3 us (93%)
  local copies, waits for them, and re-layouts  2.9 us (5%)
  between operations  0.66 us (1%)
    pallas_call x1, Pallas kernels, per_device(): pl.pallas_call(main_kernel, out_shape=(jax.ShapeDtypeStruct((4, ROWS), f3...  48.3 us
    pallas_call x1, Pallas kernels, per_device(): pl.pallas_call(pick_kernel, out_shape=jax.ShapeDtypeStruct((8, WIDTH), jn...  2.04 us
    unnamed x3, local copies, waits for them, and re-layouts  1.48 us
    slice x2, local copies, waits for them, and re-layouts, per_device(): return (out[3], out[:3], best[:STEPS, 0])  1.42 us

profile of v1, /device:TPU:1, one launch (start us, length us, event | category | flops | bytes accessed | tf_op | source)
XLA Modules:
  0.0 53.9 jit_solution(3242406180738629251)
XLA Ops:
  0.6 2.0 %pick.1.rows_ref = f32[8,256]{1,0:T(8,128)} custom-call(s32[3]{0:T(128)} %win_ref.1, bf16[32768,256]{1,0:T(8,128)(2,1)} %emb_ref.3), custom_call_target="tpu_custom_call" | custom-call | tf_op jit(solution)/shard_map/pick/pallas_call | solution.py:277
  2.7 0.0 copy-start
  2.7 0.7 %copy-done = f32[8,256]{1,0:T(8,128)S(1)} copy-done((f32[8,256]{1,0:T(8,128)S(1)}, f32[8,256]{1,0:T(8,128)}, u32[]{:S(2)}) %copy-start) | copy-done | bytes 8216
  3.4 48.3 %main.1 = (f32[4,32768]{1,0:T(4,128)S(1)}, f32[8,128]{1,0:T(8,128)S(1)}) custom-call(f32[8,256]{1,0:T(8,128)S(1)} %copy-done, bf16[32768,256]{1,0:T(8,128)(2,1)} %emb_ref.3), custom_call_target="tpu_custom_call" | custom-call | tf_op jit(solution)/shard_map/main/pallas_call | solution.py:288
  51.7 0.6 %slice_reduce_fusion = f32[3]{0:T(128)} fusion(f32[8,128]{1,0:T(8,128)S(1)} %get-tuple-element.6), kind=kLoop, calls=%fused_computation | loop fusion | bytes 24 | tf_op jit(solution)/shard_map/slice | solution.py:322
  52.3 0.8 %slice.9 = f32[1,32768]{1,0:T(1,128)} slice(f32[4,32768]{1,0:T(4,128)S(1)} %get-tuple-element.5), slice={[3:4], [0:32768]} | slice | bytes 262144 | tf_op jit(solution)/shard_map/slice | solution.py:322
  53.1 0.8 %copy.6 = f32[3,32768]{1,0:T(4,128)} copy(f32[3,32768]{1,0:T(4,128)S(1)} %bitcast.2) | data formatting | bytes 786432
Async XLA Ops:
  2.7 0.7 %copy-start = (f32[8,256]{1,0:T(8,128)S(1)}, f32[8,256]{1,0:T(8,128)}, u32[]{:S(2)}) copy-start(f32[8,256]{1,0:T(8,128)} %pick.1.rows_ref) | copy-start | bytes 24580
